TPU v7x, 32 devices: a whole 2x2x4 slice. The times are simulated.
32 devices in a mesh: cluster: 8 (over z, x), sub: 4 (over y, core).
Axes of the slice: x: 2, y: 2, z: 4, core: 2. Of those that a mesh axis runs over, the one named last changes fastest.
Arguments:
- mantissas: int32 [8, 64, 168, 128], P('cluster', 'sub'), may hold values from -128 to 127
- exponents: int32 [8, 64, 14], P('cluster', 'sub'), may hold values from -9 to -6
- channel: bfloat16 [8, 64, 2, 64, 128], P('cluster', 'sub'), may hold values from -0.5 to 0.5
- inverses: bfloat16 [8, 64, 2, 128, 128], P('cluster', 'sub'), may hold values from -4 to 4, as said below
Outputs:
- detected: bfloat16 [64, 168, 256], P('sub')
Inputs may be any that keep to these rules, and one draw needn't show every extreme that they name: `inverses`: each real part has a positive diagonal; the matrices are otherwise dense.
All inputs are finite; a program needn't handle non-finite values.
Results may differ from a plain program's by a relative error of at most 0.0074.
Values may be sent and summed in bfloat16 or wider, within the bound.
A program may use at most 64 MiB of HBM per device.

v0:
```python
import jax
import jax.numpy as jnp
from jax import lax
from jax.sharding import PartitionSpec as P

ITERS = 3


RHO = 0.5


def complex_block(real, imag):
    top = jnp.concatenate([real, -imag], axis=-1)
    bottom = jnp.concatenate([imag, real], axis=-1)
    return jnp.concatenate([top, bottom], axis=-2)


def per_device(mantissas, exponents, channel, inverses):
    clusters = lax.axis_size("cluster")
    mant = mantissas[0]
    blocks, vectors, _ = mant.shape
    expo = exponents[0]
    scale = jnp.repeat(jnp.exp2(expo.astype(jnp.float32)), vectors // expo.shape[1], axis=1)
    signal = (mant.astype(jnp.float32) * scale[:, :, None]).astype(jnp.bfloat16)
    match = complex_block(channel[0, :, 0], channel[0, :, 1])
    matched_filter = jnp.einsum("rsa,rau->rsu", signal, match, preferred_element_type=jnp.float32)
    solve_block = complex_block(inverses[0, :, 0], inverses[0, :, 1])
    width = matched_filter.shape[2]
    consensus = jnp.zeros(matched_filter.shape, jnp.float32)
    dual = jnp.zeros(matched_filter.shape, jnp.float32)
    for step in range(ITERS):
        rhs = (matched_filter + RHO * (consensus - dual)).astype(jnp.bfloat16)
        local = jnp.einsum("rsk,rjk->rsj", rhs, solve_block, preferred_element_type=jnp.float32)
        term = local + dual
        flat = term.reshape(blocks * vectors, width)
        share = lax.psum_scatter(flat, "cluster", scatter_dimension=0, tiled=True)
        average = (share / clusters).astype(jnp.bfloat16)
        gathered = lax.all_gather(average, "cluster", axis=0, tiled=True)
        consensus = gathered.reshape(blocks, vectors, width).astype(jnp.float32)
        dual = term - consensus
    users = width // 2
    column_list = jnp.sum(consensus * consensus, axis=(0, 1))
    partial_value = column_list[:users] + column_list[users:]
    total_power = lax.psum(partial_value, "sub")
    power = total_power / (blocks * lax.axis_size("sub") * vectors)
    factor = lax.rsqrt(power + 1e-06)
    factor = jnp.concatenate([factor, factor])
    return (consensus * factor).astype(jnp.bfloat16)


def solution(mesh):
    placed = (
        P("cluster", "sub", None, None),
        P("cluster", "sub", None),
        P("cluster", "sub", None, None, None),
        P("cluster", "sub", None, None, None),
    )
    return jax.shard_map(
        per_device, mesh=mesh, in_specs=placed, out_specs=P("sub", None, None), check_vma=False
    )
```

profile of v0, /device:TPU:0, one launch (start us, length us, event | category | flops | bytes accessed | tf_op | source)
XLA Modules:
  0.0 393.4 jit_solution(11023630587310864629)
XLA Ops:
  6.5 0.0 copy-start
  6.5 0.0 copy-start.4
  6.5 0.0 reduce-scatter.4.cloned.1.call-start
  6.5 1.1 fusion.28
  7.6 1.1 slice_bitcast_fusion.2
  8.7 1.9 fusion.29
  10.6 0.0 copy-done
  10.6 1.1 slice_bitcast_fusion
  11.7 0.0 copy-done.4
  11.7 0.1 copy.15
  11.8 0.1 broadcast_in_dim.4
  11.9 0.1 mul.28
  12.0 0.0 copy-start.2
  12.0 0.0 copy-start.3
  12.0 2.0 fusion.15
  14.0 0.0 copy-done.2
  14.0 0.0 copy-done.3
  14.1 3.5 fusion.13
  17.6 0.0 copy-start.1
  17.6 0.0 reduce-scatter.4.cloned.1.call-update
  17.6 0.0 all-gather.4.cloned.1.call-start
  17.6 74.6 %reduce-scatter.4.cloned.1.call-done = f32[336,256]{1,0:T(8,128)} async-done(((f32[2688,256]{1,0:T(8,128)}), f32[336,256]{1,0:T(8,128)}) %reduce-scatter.4.cloned.1.call-update) | async-done | bytes 344080 | tf_op jit(solution)/shard_map/reduce_scatter | solution.py:36
  92.2 1.7 multiply_convert_fusion.3
  93.9 0.0 all-gather.4.cloned.1.call-update
  93.9 0.0 reduce-scatter.6.cloned.1.call-start
  94.0 41.8 %all-gather.4.cloned.1.call-done = bf16[2688,256]{1,0:T(8,128)(2,1)} async-done(((bf16[336,256]{1,0:T(8,128)(2,1)}), bf16[2688,256]{1,0:T(8,128)(2,1)}) %all-gather.4.cloned.1.call-update) | async-done | bytes 1376272 | tf_op jit(solution)/shard_map/all_gather | solution.py:38
  135.7 0.0 copy-done.1
  135.8 6.5 %fusion.6 = f32[16,168,256]{2,1,0:T(8,128)} fusion(f32[16,168,256]{2,1,0:T(8,128)} %fusion.13, bf16[16,168,256]{2,1,0:T(8,128)(2,1)} %bitcast.41, f32[16,168,256]{2,1,0:T(8,128)S(1)} %fusion.15, bf16[16,128,128]{2,1,0:T(8,128)(2,1)} %get-tuple-element.6, bf16[16,128,128]{2,1,0:T(8,128)(2,1)} %get-tuple-element.5, bf16[16,128,128]{2,1,0:T(8,128)(2,1)S(1)} %copy-done.1), kind=kOutput, calls=%fused_computation.12 | convolution fusion | flops 366903296 | bytes 11206656 | tf_op jit(solution)/shard_map/rsk,rjk->rsj/dot_general | solution.py:33
  142.2 0.0 reduce-scatter.6.cloned.1.call-update
  142.2 0.0 all-gather.6.cloned.1.call-start
  142.3 70.3 %reduce-scatter.6.cloned.1.call-done = f32[336,256]{1,0:T(8,128)} async-done(((f32[2688,256]{1,0:T(8,128)}), f32[336,256]{1,0:T(8,128)}) %reduce-scatter.6.cloned.1.call-update) | async-done | bytes 344080 | tf_op jit(solution)/shard_map/reduce_scatter | solution.py:36
  212.6 1.7 multiply_convert_fusion.2
  214.3 0.0 all-gather.6.cloned.1.call-update
  214.3 0.0 reduce-scatter.8.cloned.1.call-start
  214.4 41.6 %all-gather.6.cloned.1.call-done = bf16[2688,256]{1,0:T(8,128)(2,1)} async-done(((bf16[336,256]{1,0:T(8,128)(2,1)}), bf16[2688,256]{1,0:T(8,128)(2,1)}) %all-gather.6.cloned.1.call-update) | async-done | bytes 1376272 | tf_op jit(solution)/shard_map/all_gather | solution.py:38
  256.0 6.4 %fusion.7 = f32[16,168,256]{2,1,0:T(8,128)} fusion(f32[16,168,256]{2,1,0:T(8,128)} %fusion.6, bf16[16,168,256]{2,1,0:T(8,128)(2,1)} %bitcast.40, f32[16,168,256]{2,1,0:T(8,128)S(1)} %fusion.15, bf16[16,128,128]{2,1,0:T(8,128)(2,1)} %get-tuple-element.6, bf16[16,128,128]{2,1,0:T(8,128)(2,1)} %get-tuple-element.5, bf16[16,128,128]{2,1,0:T(8,128)(2,1)S(1)} %copy-done.1), kind=kOutput, calls=%fused_computation.13 | convolution fusion | flops 366903296 | bytes 11206656 | tf_op jit(solution)/shard_map/rsk,rjk->rsj/dot_general | solution.py:33
  262.4 0.0 reduce-scatter.8.cloned.1.call-update
  262.4 0.0 all-gather.8.cloned.1.call-start
  262.4 70.7 %reduce-scatter.8.cloned.1.call-done = f32[336,256]{1,0:T(8,128)} async-done(((f32[2688,256]{1,0:T(8,128)}), f32[336,256]{1,0:T(8,128)}) %reduce-scatter.8.cloned.1.call-update) | async-done | bytes 344080 | tf_op jit(solution)/shard_map/reduce_scatter | solution.py:36
  333.2 1.7 multiply_convert_fusion.1
  334.9 0.0 all-gather.8.cloned.1.call-update
  334.9 41.6 %all-gather.8.cloned.1.call-done = bf16[2688,256]{1,0:T(8,128)(2,1)} async-done(((bf16[336,256]{1,0:T(8,128)(2,1)}), bf16[2688,256]{1,0:T(8,128)(2,1)}) %all-gather.8.cloned.1.call-update) | async-done | bytes 1376272 | tf_op jit(solution)/shard_map/all_gather | solution.py:38
  376.5 1.7 multiply_reduce_fusion
  378.2 5.7 %psum.7 = f32[128]{0:T(128)S(1)} all-reduce(f32[128]{0:T(128)S(1)} %slice_add_fusion), channel_id=1, replica_groups=mesh['cluster'=8,'sub'=4] {'sub'}, use_global_device_ids=true, to_apply=%region_4.0 | all-reduce | flops 128 | bytes 1024 | tf_op jit(solution)/shard_map/psum | solution.py:44
  383.9 2.7 multiply_convert_fusion
  (4 shorter events, 0.0 us)
Async XLA Ops:
  6.5 4.1 %copy-start = (bf16[1,16,2,128,128]{4,3,2,1,0:T(8,128)(2,1)S(1)}, bf16[1,16,2,128,128]{4,3,2,1,0:T(8,128)(2,1)}, u32[]{:S(2)}) copy-start(bf16[1,16,2,128,128]{4,3,2,1,0:T(8,128)(2,1)} %param.7) | copy-start | bytes 3145732
  6.5 5.2 %copy-start.4 = (s32[1,16,14]{1,0,2:T(1,128)S(1)}, s32[1,16,14]{1,0,2:T(1,128)}, u32[]{:S(2)}) copy-start(s32[1,16,14]{1,0,2:T(1,128)} %param.5) | copy-start | bytes 2692
  6.5 85.7 %reduce-scatter.4.cloned.1.call-start = ((), (), s32[]{:S(2)}) async-start(), calls=%async_computation.3 | async-start | bytes 3096576 | tf_op jit(solution)/shard_map/reduce_scatter | solution.py:36
  12.0 2.0 copy-start.2
  12.0 2.0 copy-start.3
  17.6 118.2 %copy-start.1 = (bf16[16,128,128]{2,1,0:T(8,128)(2,1)S(1)}, bf16[16,128,128]{2,1,0:T(8,128)(2,1)}, u32[]{:S(2)}) copy-start(bf16[16,128,128]{2,1,0:T(8,128)(2,1)} %fusion.29) | copy-start | bytes 1572868
  17.6 118.2 %all-gather.4.cloned.1.call-start = ((), (), s32[]{:S(2)}) async-start(), calls=%async_computation.4 | async-start | bytes 1548288 | tf_op jit(solution)/shard_map/all_gather | solution.py:38
  93.9 118.7 %reduce-scatter.6.cloned.1.call-start = ((), (), s32[]{:S(2)}) async-start(), calls=%async_computation.5 | async-start | bytes 3096576 | tf_op jit(solution)/shard_map/reduce_scatter | solution.py:36
  142.2 113.7 %all-gather.6.cloned.1.call-start = ((), (), s32[]{:S(2)}) async-start(), calls=%async_computation.6 | async-start | bytes 1548288 | tf_op jit(solution)/shard_map/all_gather | solution.py:38
  214.3 118.9 %reduce-scatter.8.cloned.1.call-start = ((), (), s32[]{:S(2)}) async-start(), calls=%async_computation.7 | async-start | bytes 3096576 | tf_op jit(solution)/shard_map/reduce_scatter | solution.py:36
  262.4 114.1 %all-gather.8.cloned.1.call-start = ((), (), s32[]{:S(2)}) async-start(), calls=%async_computation.8 | async-start | bytes 1548288 | tf_op jit(solution)/shard_map/all_gather | solution.py:38
Sparse Core Ops, SparseCore 0:
  17.7 74.4 reduce-scatter.3
  94.4 41.2 all-gather.3
  142.4 70.2 reduce-scatter.5
  214.7 41.2 all-gather.5
  262.5 70.6 reduce-scatter.7
  335.2 41.2 all-gather.7
where the time goes:
time: 394 us; the launch traced here: 393 us
  waiting for transfers between devices  341 us (87%)
  matrix products  18.4 us (5%)
  between operations  13.5 us (3%)
  other arithmetic  12.4 us (3%)
  blocking collectives  5.66 us (1%)
    reduce_scatter x3, waiting for transfers between devices, per_device(): share = lax.psum_scatter(flat, 'cluster', scatter_dimension=0, tiled=True)  216 us
    all_gather x3, waiting for transfers between devices, per_device(): gathered = lax.all_gather(average, 'cluster', axis=0, tiled=True)  125 us
    dot_general x3, matrix products, per_device(): jnp.einsum('rsk,rjk->rsj', rhs, solve_block, preferred_element_type=jnp.f...  16.4 us
  transfers between devices with their start and end apart: 6, of which 6 were waited for; matrix products, arithmetic and copies ran while one was open for 0% of the time, Pallas kernels for 0%

commit v1 on v0

--- a/solution.py
+++ b/solution.py
@@ -1,12 +1,17 @@
+import functools
+
 import jax
 import jax.numpy as jnp
 from jax import lax
+from jax.experimental import pallas as pl
+from jax.experimental.pallas import tpu as pltpu
 from jax.sharding import PartitionSpec as P
 
 ITERS = 3
 
 
 RHO = 0.5
+MESH = pl.DeviceIdType.MESH
 
 
 def complex_block(real, imag):
@@ -15,7 +20,7 @@
     return jnp.concatenate([top, bottom], axis=-2)
 
 
-def per_device(mantissas, exponents, channel, inverses):
+def reduce_plan(mantissas, exponents, channel, inverses):
     clusters = lax.axis_size("cluster")
     mant = mantissas[0]
     blocks, vectors, _ = mant.shape
@@ -48,7 +53,258 @@
     return (consensus * factor).astype(jnp.bfloat16)
 
 
+def kernel(
+    n, subs,
+    mant_hbm, expo_ref, chan_hbm, inv_hbm,
+    out_ref, factor_ref,
+    mant_v, sig_v, r_sig, r_chan, r_inv, match_v, solve_v, matched_v, term_v, cons_v, power_v, r_pow, r_sub,
+    local_sem, own_sem, send_sem, recv_sem, ag_send, ag_recv, fw_send, fw_recv, pw_send, pw_recv, sb_send, sb_recv,
+):
+    me = lax.axis_index("cluster")
+    my_sub = lax.axis_index("sub")
+    blocks, vectors, ants = mant_v.shape
+    per = blocks // n
+    symbols = expo_ref.shape[2]
+    tones = vectors // symbols
+    half = ants // 2
+    users = chan_hbm.shape[4]
+    width = 2 * users
+    partner = me + 1 - 2 * lax.rem(me, 2)
+
+    def peer(off):
+        return lax.rem(me + off, n)
+
+    def source(off):
+        return lax.rem(me + n - off, n)
+
+    def remote(src, dst, send, recv, where):
+        return pltpu.make_async_remote_copy(
+            src_ref=src, dst_ref=dst, send_sem=send, recv_sem=recv, device_id=where, device_id_type=MESH
+        )
+
+    def deal(kind, off, b):
+        index = peer(off) * per + b
+        src, dst = (
+            (inv_hbm.at[0, index], r_inv.at[off, b]),
+            (chan_hbm.at[0, index], r_chan.at[off, b]),
+            (sig_v.at[index], r_sig.at[off, b]),
+        )[kind]
+        return remote(src, dst, send_sem.at[kind, off, b], recv_sem.at[kind, off, b], {"cluster": peer(off)})
+
+    def own(kind, b):
+        index = me * per + b
+        src, dst = (
+            (inv_hbm.at[0, index], r_inv.at[0, b]),
+            (chan_hbm.at[0, index], r_chan.at[0, b]),
+        )[kind]
+        return pltpu.make_async_copy(src, dst, own_sem.at[kind, b])
+
+    def gather(off, b):
+        slot = out_ref.at[me * per + b]
+        return remote(slot, slot, ag_send.at[off, b], ag_recv.at[off, b], {"cluster": peer(off)})
+
+    def gather_partner(b):
+        slot = out_ref.at[me * per + b]
+        return remote(slot, slot, ag_send.at[0, b], ag_recv.at[0, b], {"cluster": partner})
+
+    def forward(off, b):
+        slot = out_ref.at[source(off) * per + b]
+        return remote(slot, slot, fw_send.at[off, b], fw_recv.at[off, b], {"cluster": partner})
+
+    def share_power(off):
+        slot = r_pow.at[me]
+        return remote(slot, slot, pw_send.at[off], pw_recv.at[off], {"cluster": peer(off)})
+
+    def share_sub(off):
+        slot = r_sub.at[my_sub]
+        return remote(slot, slot, sb_send.at[off], sb_recv.at[off], {"sub": lax.rem(my_sub + off, subs)})
+
+    load = pltpu.make_async_copy(mant_hbm.at[0], mant_v, local_sem)
+    load.start()
+    for b in range(per):
+        own(0, b).start()
+        own(1, b).start()
+    barrier = pltpu.get_barrier_semaphore()
+    for off in range(1, n):
+        pl.semaphore_signal(barrier, inc=1, device_id={"cluster": peer(off)}, device_id_type=MESH)
+    for off in range(1, subs):
+        pl.semaphore_signal(
+            barrier, inc=1, device_id={"sub": lax.rem(my_sub + off, subs)}, device_id_type=MESH
+        )
+    pl.semaphore_wait(barrier, n - 1 + subs - 1)
+
+    for off in range(1, n):
+        deal(1, off, 0).start()
+        deal(0, off, 0).start()
+    row = lax.broadcasted_iota(jnp.int32, (vectors, symbols), 0)
+    first = lax.broadcasted_iota(jnp.int32, (vectors, symbols), 1) * tones
+    spread = jnp.where((row >= first) & (row < first + tones), 1.0, 0.0).astype(jnp.bfloat16)
+    steps = jnp.exp2(expo_ref[0].astype(jnp.float32)).astype(jnp.bfloat16)
+    scale = lax.dot_general(spread, steps, (((1,), (1,)), ((), ())), preferred_element_type=jnp.float32)
+    load.wait()
+    for b in range(per):
+        for p in range(n):
+            g = p * per + b
+            sig_v[g] = (mant_v[g].astype(jnp.float32) * scale[:, g : g + 1]).astype(jnp.bfloat16)
+        for off in range(1, n):
+            if b > 0:
+                deal(1, off, b).start()
+                deal(0, off, b).start()
+            deal(2, off, b).start()
+    power_v[...] = jnp.zeros_like(power_v)
+
+    def solve(rhs, off):
+        return lax.dot_general(
+            rhs.astype(jnp.bfloat16), solve_v[off], (((1,), (1,)), ((), ())), preferred_element_type=jnp.float32
+        )
+
+    def one_slot(b, carry):
+        total = None
+        for off in range(n):
+            if off == 0:
+                own(0, b).wait()
+                own(1, b).wait()
+                signal = sig_v[me * per + b]
+            else:
+                for kind in range(3):
+                    deal(kind, off, b).wait_recv()
+                signal = r_sig[off, b]
+            real, imag = r_chan[off, b, 0], r_chan[off, b, 1]
+            match_v[off, :half, :users] = real
+            match_v[off, :half, users:] = -imag
+            match_v[off, half:, :users] = imag
+            match_v[off, half:, users:] = real
+            real, imag = r_inv[off, b, 0], r_inv[off, b, 1]
+            solve_v[off, :users, :users] = real
+            solve_v[off, :users, users:] = -imag
+            solve_v[off, users:, :users] = imag
+            solve_v[off, users:, users:] = real
+            matched = jnp.dot(signal, match_v[off], preferred_element_type=jnp.float32)
+            matched_v[off] = matched
+            term = solve(matched, off)
+            term_v[off] = term
+            total = term if total is None else total + term
+        for step in range(1, ITERS):
+            cons_v[...] = (total / n).astype(jnp.bfloat16).astype(jnp.float32)
+            total = None
+            for off in range(n):
+                consensus = cons_v[...]
+                dual = term_v[off] - consensus
+                term = solve(matched_v[off] + RHO * (consensus - dual), off) + dual
+                if step < ITERS - 1:
+                    term_v[off] = term
+                total = term if total is None else total + term
+        final = (total / n).astype(jnp.bfloat16)
+        out_ref[me * per + b] = final
+        final = final.astype(jnp.float32)
+        columns = jnp.sum(final * final, axis=0, keepdims=True)
+        power_v[...] += columns[:, :users] + columns[:, users:]
+        for off in range(2, n, 2):
+            gather(off, b).start()
+        gather_partner(b).start()
+        return carry
+
+    lax.fori_loop(0, per, one_slot, 0)
+
+    r_pow[me] = power_v[...]
+    for off in range(1, n):
+        share_power(off).start()
+    for off in range(1, n):
+        share_power(off).wait_recv()
+    r_sub[my_sub] = jnp.sum(r_pow[...], axis=0)
+    for off in range(1, subs):
+        share_sub(off).start()
+    for b in range(per):
+        for off in range(2, n, 2):
+            gather(off, b).wait_recv()
+            forward(off, b).start()
+    for off in range(1, subs):
+        share_sub(off).wait_recv()
+    power = jnp.sum(r_sub[...], axis=0) / (blocks * subs * vectors)
+    factor = lax.rsqrt(power + 1e-06)
+    factor_ref[:, :users] = factor
+    factor_ref[:, users:] = factor
+    for b in range(per):
+        for off in range(1, n):
+            for kind in range(3):
+                deal(kind, off, b).wait_send()
+        gather_partner(b).wait()
+        for off in range(2, n, 2):
+            gather(off, b).wait_send()
+            forward(off, b).wait()
+    for off in range(1, n):
+        share_power(off).wait_send()
+    for off in range(1, subs):
+        share_sub(off).wait_send()
+
+
+def regroup_plan(n, subs, mantissas, exponents, channel, inverses):
+    _, blocks, vectors, ants = mantissas.shape
+    users = channel.shape[4]
+    width = 2 * users
+    per = blocks // n
+    flops = 2 * blocks * vectors * width * (ants + ITERS * width)
+    dma = pltpu.SemaphoreType.DMA
+    consensus, factor = pl.pallas_call(
+        functools.partial(kernel, n, subs),
+        out_shape=(
+            jax.ShapeDtypeStruct((blocks, vectors, width), jnp.bfloat16),
+            jax.ShapeDtypeStruct((1, width), jnp.float32),
+        ),
+        in_specs=[
+            pl.BlockSpec(memory_space=pl.ANY),
+            pl.BlockSpec(memory_space=pltpu.VMEM),
+            pl.BlockSpec(memory_space=pl.ANY),
+            pl.BlockSpec(memory_space=pl.ANY),
+        ],
+        out_specs=(
+            pl.BlockSpec(memory_space=pltpu.VMEM),
+            pl.BlockSpec(memory_space=pltpu.VMEM),
+        ),
+        scratch_shapes=[
+            pltpu.VMEM((blocks, vectors, ants), jnp.int32),
+            pltpu.VMEM((blocks, vectors, ants), jnp.bfloat16),
+            pltpu.VMEM((n, per, vectors, ants), jnp.bfloat16),
+            pltpu.VMEM((n, per) + channel.shape[2:], jnp.bfloat16),
+            pltpu.VMEM((n, per) + inverses.shape[2:], jnp.bfloat16),
+            pltpu.VMEM((n, ants, width), jnp.bfloat16),
+            pltpu.VMEM((n, width, width), jnp.bfloat16),
+            pltpu.VMEM((n, vectors, width), jnp.float32),
+            pltpu.VMEM((n, vectors, width), jnp.float32),
+            pltpu.VMEM((vectors, width), jnp.float32),
+            pltpu.VMEM((1, users), jnp.float32),
+            pltpu.VMEM((n, 1, users), jnp.float32),
+            pltpu.VMEM((subs, 1, users), jnp.float32),
+            dma,
+            dma((2, per)),
+            dma((3, n, per)),
+            dma((3, n, per)),
+            dma((n, per)),
+            dma((n, per)),
+            dma((n, per)),
+            dma((n, per)),
+            dma((n,)),
+            dma((n,)),
+            dma((subs,)),
+            dma((subs,)),
+        ],
+        compiler_params=pltpu.CompilerParams(
+            collective_id=0, has_side_effects=True, vmem_limit_bytes=48 * 1024 * 1024
+        ),
+        cost_estimate=pl.CostEstimate(flops=flops, bytes_accessed=8 * blocks * vectors * width, transcendentals=0),
+    )(mantissas, exponents, channel, inverses)
+    return (consensus.astype(jnp.float32) * factor[None]).astype(jnp.bfloat16)
+
+
 def solution(mesh):
+    n, subs = mesh.shape["cluster"], mesh.shape["sub"]
+
+    def per_device(mantissas, exponents, channel, inverses):
+        blocks = mantissas.shape[1]
+        if n % 2 == 0 and blocks % n == 0:
+            return regroup_plan(n, subs, mantissas, exponents, channel, inverses)
+        return reduce_plan(mantissas, exponents, channel, inverses)
+
     placed = (
         P("cluster", "sub", None, None),
         P("cluster", "sub", None),

time: 394 us -> 91.3 us (0.23)
  waiting for transfers between devices: 341 us -> 0 us
  Pallas kernels: 0 us -> 85.3 us
  matrix products: 18.4 us -> 0 us
  between operations: 13.5 us -> 0.01 us
  other arithmetic: 12.4 us -> 1.4 us
  blocking collectives: 5.66 us -> 0 us
    reduce_scatter x3 -> x0, waiting for transfers between devices: 216 us -> none  [per_device(): share = lax.psum_scatter(flat, 'cluster', scatter_dimension=0, tiled=True)]
    all_gather x3 -> x0, waiting for transfers between devices: 125 us -> none  [per_device(): gathered = lax.all_gather(average, 'cluster', axis=0, tiled=True)]
    pallas_call x0 -> x1, Pallas kernels: none -> 85.3 us  [regroup_plan(): pl.pallas_call(functools.partial(kernel, n, subs), out_shape=(jax.ShapeDt...]
    dot_general x4 -> x0, matrix products: 18.4 us -> none  [the longest x3 16.4 us: per_device(): jnp.einsum('rsk,rjk->rsj', rhs, solve_block, preferred_element_type=jnp.f...]
    convert_element_type x4 -> x1, other arithmetic: 7.68 us -> 1.4 us  [regroup_plan(): return (consensus.astype(jnp.float32) * factor[None]).astype(jnp.bfloat16)]
    psum x1 -> x0, blocking collectives: 5.66 us -> none  [per_device(): total_power = lax.psum(partial_value, 'sub')]
    unnamed x10 -> x7, local copies, waits for them, and re-layouts: 0.02 us -> 4.37 us
  transfers between devices with their start and end apart: 6 -> 0, of which waited for: 6 -> 0; matrix products, arithmetic and copies ran while one was open for 0% -> 0% of each run, Pallas kernels for 0% -> 0%
where the time goes in v1:
time: 91.3 us; the launch traced here: 91.1 us
  Pallas kernels  85.3 us (93%)
  local copies, waits for them, and re-layouts  4.37 us (5%)
  other arithmetic  1.4 us (2%)
    pallas_call x1, Pallas kernels, regroup_plan(): pl.pallas_call(functools.partial(kernel, n, subs), out_shape=(jax.ShapeDt...  85.3 us
    unnamed x7, local copies, waits for them, and re-layouts  4.37 us

profile of v1, /device:TPU:0, one launch (start us, length us, event | category | flops | bytes accessed | tf_op | source)
XLA Modules:
  0.0 91.1 jit_solution(15638027799158123997)
XLA Ops:
  0.0 0.8 copy.5.expo_ref
  0.8 0.0 copy-start
  0.8 1.3 %copy-done = s32[1,16,168,128]{3,2,1,0:T(8,128)S(1)} copy-done((s32[1,16,168,128]{3,2,1,0:T(8,128)S(1)}, s32[1,16,168,128]{3,2,1,0:T(8,128)}, u32[]{:S(2)}) %copy-start) | copy-done | bytes 1376280
  2.1 0.0 copy-start.1
  2.1 1.2 %copy-done.1 = bf16[1,16,2,128,128]{4,3,2,1,0:T(8,128)(2,1)S(1)} copy-done((bf16[1,16,2,128,128]{4,3,2,1,0:T(8,128)(2,1)S(1)}, bf16[1,16,2,128,128]{4,3,2,1,0:T(8,128)(2,1)}, u32[]{:S(2)}) %copy-start.1) | copy-done | bytes 1048600
  3.3 0.0 copy-start.2
  3.3 1.0 %copy-done.2 = bf16[1,16,2,64,128]{4,3,2,1,0:T(8,128)(2,1)S(1)} copy-done((bf16[1,16,2,64,128]{4,3,2,1,0:T(8,128)(2,1)S(1)}, bf16[1,16,2,64,128]{4,3,2,1,0:T(8,128)(2,1)}, u32[]{:S(2)}) %copy-start.2) | copy-done | bytes 524312
  4.4 85.3 %shard_map.46 = (bf16[16,168,256]{2,1,0:T(8,128)(2,1)S(1)}, f32[1,256]{1,0:T(1,128)S(1)}) custom-call(s32[1,16,168,128]{3,2,1,0:T(8,128)S(1)} %copy-done, s32[1,16,14]{2,1,0:T(8,128)S(1)} %copy.5.expo_ref, bf16[1,16,2,64,128]{4,3,2,1,0:T(8,128)(2,1)S(1)} %copy-done.2, bf16[1,16,2,128,128]{4,3,2,1,0:T(8,128)(2,1)S(1)} %copy-done.1), custom_call_target="tpu_custom_call" | custom-call | flops 1233125376 | bytes 5505024 | tf_op jit(solution)/shard_map/pallas_call | solution.py:248
  89.7 1.4 %multiply_convert_fusion = bf16[16,168,256]{2,1,0:T(8,128)(2,1)} fusion(bf16[16,168,256]{2,1,0:T(8,128)(2,1)S(1)} %get-tuple-element.7, f32[256]{0:T(256)S(1)} %bitcast.1), kind=kLoop, calls=%fused_computation | loop fusion | flops 2064384 | bytes 2753536 | tf_op jit(solution)/shard_map/convert_element_type | solution.py:296
Async XLA Ops:
  0.8 1.3 %copy-start = (s32[1,16,168,128]{3,2,1,0:T(8,128)S(1)}, s32[1,16,168,128]{3,2,1,0:T(8,128)}, u32[]{:S(2)}) copy-start(s32[1,16,168,128]{3,2,1,0:T(8,128)} %mant_hbm.1) | copy-start | bytes 4128772
  2.1 1.2 %copy-start.1 = (bf16[1,16,2,128,128]{4,3,2,1,0:T(8,128)(2,1)S(1)}, bf16[1,16,2,128,128]{4,3,2,1,0:T(8,128)(2,1)}, u32[]{:S(2)}) copy-start(bf16[1,16,2,128,128]{4,3,2,1,0:T(8,128)(2,1)} %inv_hbm.1) | copy-start | bytes 3145732
  3.3 1.0 %copy-start.2 = (bf16[1,16,2,64,128]{4,3,2,1,0:T(8,128)(2,1)S(1)}, bf16[1,16,2,64,128]{4,3,2,1,0:T(8,128)(2,1)}, u32[]{:S(2)}) copy-start(bf16[1,16,2,64,128]{4,3,2,1,0:T(8,128)(2,1)} %chan_hbm.1) | copy-start | bytes 1572868

commit v2 on v1

v2 whole, which is shorter than its diff:
```python
import functools

import jax
import jax.numpy as jnp
from jax import lax
from jax.experimental import pallas as pl
from jax.experimental.pallas import tpu as pltpu
from jax.sharding import PartitionSpec as P

ITERS = 3


RHO = 0.5
MESH = pl.DeviceIdType.MESH


def complex_block(real, imag):
    top = jnp.concatenate([real, -imag], axis=-1)
    bottom = jnp.concatenate([imag, real], axis=-1)
    return jnp.concatenate([top, bottom], axis=-2)


def reduce_plan(mantissas, exponents, channel, inverses):
    clusters = lax.axis_size("cluster")
    mant = mantissas[0]
    blocks, vectors, _ = mant.shape
    expo = exponents[0]
    scale = jnp.repeat(jnp.exp2(expo.astype(jnp.float32)), vectors // expo.shape[1], axis=1)
    signal = (mant.astype(jnp.float32) * scale[:, :, None]).astype(jnp.bfloat16)
    match = complex_block(channel[0, :, 0], channel[0, :, 1])
    matched_filter = jnp.einsum("rsa,rau->rsu", signal, match, preferred_element_type=jnp.float32)
    solve_block = complex_block(inverses[0, :, 0], inverses[0, :, 1])
    width = matched_filter.shape[2]
    consensus = jnp.zeros(matched_filter.shape, jnp.float32)
    dual = jnp.zeros(matched_filter.shape, jnp.float32)
    for step in range(ITERS):
        rhs = (matched_filter + RHO * (consensus - dual)).astype(jnp.bfloat16)
        local = jnp.einsum("rsk,rjk->rsj", rhs, solve_block, preferred_element_type=jnp.float32)
        term = local + dual
        flat = term.reshape(blocks * vectors, width)
        share = lax.psum_scatter(flat, "cluster", scatter_dimension=0, tiled=True)
        average = (share / clusters).astype(jnp.bfloat16)
        gathered = lax.all_gather(average, "cluster", axis=0, tiled=True)
        consensus = gathered.reshape(blocks, vectors, width).astype(jnp.float32)
        dual = term - consensus
    users = width // 2
    column_list = jnp.sum(consensus * consensus, axis=(0, 1))
    partial_value = column_list[:users] + column_list[users:]
    total_power = lax.psum(partial_value, "sub")
    power = total_power / (blocks * lax.axis_size("sub") * vectors)
    factor = lax.rsqrt(power + 1e-06)
    factor = jnp.concatenate([factor, factor])
    return (consensus * factor).astype(jnp.bfloat16)


def lowest_bit(mask):
    bit = 0
    while not (mask >> bit) & 1:
        bit += 1
    return bit


def row_parts(vectors):
    cut = min(vectors, -(-vectors // 32) * 16)
    return [(0, cut)] + ([(cut, vectors - cut)] if cut < vectors else [])


def kernel(
    n, subs,
    mant_hbm, expo_ref, chan_hbm, inv_hbm,
    out_ref, factor_ref,
    mant_v, sig_v, r_sig, r_chan, r_inv, match_v, solve_v, matched_v, term_v, cons_v, power_v, r_pow, r_sub,
    local_sem, own_sem, send_sem, recv_sem, ag_send, ag_recv, pw_send, pw_recv, sb_send, sb_recv,
):
    me = lax.axis_index("cluster")
    my_sub = lax.axis_index("sub")
    blocks, vectors, ants = mant_v.shape
    per = blocks // n
    symbols = expo_ref.shape[2]
    tones = vectors // symbols
    half = ants // 2
    users = chan_hbm.shape[4]
    bits = n.bit_length() - 1
    parts = row_parts(vectors)

    def flip(mask):
        index = me
        for bit in range(bits):
            if (mask >> bit) & 1:
                index = index + (1 - 2 * lax.rem(me // 2**bit, 2)) * 2**bit
        return index

    def remote(src, dst, send, recv, where):
        return pltpu.make_async_remote_copy(
            src_ref=src, dst_ref=dst, send_sem=send, recv_sem=recv, device_id=where, device_id_type=MESH
        )

    def deal(kind, mask, b):
        index = flip(mask) * per + b
        if kind == 0:
            src, dst = inv_hbm.at[0, index], r_inv.at[mask, b]
        elif kind == 1:
            src, dst = chan_hbm.at[0, index], r_chan.at[mask, b]
        else:
            rows = pl.ds(*parts[kind - 2])
            src, dst = sig_v.at[index, rows], r_sig.at[mask, b, rows]
        return remote(src, dst, send_sem.at[kind, mask, b], recv_sem.at[kind, mask, b], {"cluster": flip(mask)})

    def own(kind, b):
        index = me * per + b
        src, dst = (
            (inv_hbm.at[0, index], r_inv.at[0, b]),
            (chan_hbm.at[0, index], r_chan.at[0, b]),
        )[kind]
        return pltpu.make_async_copy(src, dst, own_sem.at[kind, b])

    def gather(mask, b, part):
        bit = lowest_bit(mask)
        slot = out_ref.at[flip(mask - 2**bit) * per + b, pl.ds(*parts[part])]
        return remote(
            slot, slot, ag_send.at[part, mask, b], ag_recv.at[part, mask, b], {"cluster": flip(2**bit)}
        )

    def pass_on(masks, b, part):
        for mask in masks:
            gather(mask, b, part).wait_recv()
            for bit in reversed(range(lowest_bit(mask))):
                gather(mask + 2**bit, b, part).start()

    relayed = [mask for mask in range(1, n) if mask % 2 == 0]
    early = [mask for mask in relayed if mask == 2 ** lowest_bit(mask)][::-1]
    late = sorted((mask for mask in relayed if mask not in early), key=lambda m: (bin(m).count("1"), -m))
    final = [mask for mask in range(1, n) if mask % 2]

    def share_power(mask):
        slot = r_pow.at[me]
        return remote(slot, slot, pw_send.at[mask], pw_recv.at[mask], {"cluster": flip(mask)})

    def share_sub(off):
        slot = r_sub.at[my_sub]
        return remote(slot, slot, sb_send.at[off], sb_recv.at[off], {"sub": lax.rem(my_sub + off, subs)})

    load = pltpu.make_async_copy(mant_hbm.at[0], mant_v, local_sem)
    load.start()
    for b in range(per):
        own(0, b).start()
        own(1, b).start()
    barrier = pltpu.get_barrier_semaphore()
    for mask in range(1, n):
        pl.semaphore_signal(barrier, inc=1, device_id={"cluster": flip(mask)}, device_id_type=MESH)
    for off in range(1, subs):
        pl.semaphore_signal(
            barrier, inc=1, device_id={"sub": lax.rem(my_sub + off, subs)}, device_id_type=MESH
        )
    pl.semaphore_wait(barrier, n - 1 + subs - 1)

    order = [mask for bit in reversed(range(bits)) for mask in range(2**bit, 2 ** (bit + 1))]
    for mask in order:
        deal(1, mask, 0).start()
        deal(0, mask, 0).start()
    row = lax.broadcasted_iota(jnp.int32, (vectors, symbols), 0)
    first = lax.broadcasted_iota(jnp.int32, (vectors, symbols), 1) * tones
    spread = jnp.where((row >= first) & (row < first + tones), 1.0, 0.0).astype(jnp.bfloat16)
    steps = jnp.exp2(expo_ref[0].astype(jnp.float32)).astype(jnp.bfloat16)
    scale = lax.dot_general(spread, steps, (((1,), (1,)), ((), ())), preferred_element_type=jnp.float32)
    load.wait()
    for b in range(per):
        for p in range(n):
            g = p * per + b
            sig_v[g] = (mant_v[g].astype(jnp.float32) * scale[:, g : g + 1]).astype(jnp.bfloat16)
        if b > 0:
            for mask in order:
                deal(1, mask, b).start()
                deal(0, mask, b).start()
        for part in range(len(parts)):
            for mask in order:
                deal(2 + part, mask, b).start()
    power_v[...] = jnp.zeros_like(power_v)

    def solve(rhs, c):
        return lax.dot_general(
            rhs.astype(jnp.bfloat16), solve_v[c], (((1,), (1,)), ((), ())), preferred_element_type=jnp.float32
        )

    def one_slot(b, carry):
        for part, (at, count) in enumerate(parts):
            rows = pl.ds(at, count)
            total = None
            for c in [0] + order[::-1]:
                if part == 0:
                    if c == 0:
                        own(0, b).wait()
                        own(1, b).wait()
                    else:
                        deal(1, c, b).wait_recv()
                        deal(0, c, b).wait_recv()
                    real, imag = r_chan[c, b, 0], r_chan[c, b, 1]
                    match_v[c, :half, :users] = real
                    match_v[c, :half, users:] = -imag
                    match_v[c, half:, :users] = imag
                    match_v[c, half:, users:] = real
                    real, imag = r_inv[c, b, 0], r_inv[c, b, 1]
                    solve_v[c, :users, :users] = real
                    solve_v[c, :users, users:] = -imag
                    solve_v[c, users:, :users] = imag
                    solve_v[c, users:, users:] = real
                if c == 0:
                    signal = sig_v[me * per + b, rows]
                else:
                    deal(2 + part, c, b).wait_recv()
                    signal = r_sig[c, b, rows]
                matched = jnp.dot(signal, match_v[c], preferred_element_type=jnp.float32)
                matched_v[c, rows] = matched
                term = solve(matched, c)
                term_v[c, rows] = term
                total = term if total is None else total + term

            @pl.when(b > 0)
            def _():
                pass_on(early, b - 1, part)

            for step in range(1, ITERS):
                cons_v[rows] = (total / n).astype(jnp.bfloat16).astype(jnp.float32)
                total = None
                for c in range(n):
                    consensus = cons_v[rows]
                    dual = term_v[c, rows] - consensus
                    term = solve(matched_v[c, rows] + RHO * (consensus - dual), c) + dual
                    if step < ITERS - 1:
                        term_v[c, rows] = term
                    total = term if total is None else total + term
            done = (total / n).astype(jnp.bfloat16)
            out_ref[me * per + b, rows] = done
            for bit in reversed(range(bits)):
                gather(2**bit, b, part).start()
            done = done.astype(jnp.float32)
            columns = jnp.sum(done * done, axis=0, keepdims=True)
            power_v[...] += columns[:, :users] + columns[:, users:]

            @pl.when(b > 0)
            def _():
                pass_on(late, b - 1, part)

        return carry

    lax.fori_loop(0, per, one_slot, 0)

    r_pow[me] = power_v[...]
    for mask in range(1, n):
        share_power(mask).start()
    last = per - 1
    for part in range(len(parts)):
        pass_on(early, last, part)
    for mask in range(1, n):
        share_power(mask).wait_recv()
    r_sub[my_sub] = jnp.sum(r_pow[...], axis=0)
    for off in range(1, subs):
        share_sub(off).start()
    for part in range(len(parts)):
        pass_on(late, last, part)
    for off in range(1, subs):
        share_sub(off).wait_recv()
    power = jnp.sum(r_sub[...], axis=0) / (blocks * subs * vectors)
    factor = lax.rsqrt(power + 1e-06)
    factor_ref[:, :users] = factor
    factor_ref[:, users:] = factor
    for b in range(per):
        for mask in range(1, n):
            for kind in range(2 + len(parts)):
                deal(kind, mask, b).wait_send()
            for part in range(len(parts)):
                gather(mask, b, part).wait_send()
        for mask in final:
            for part in range(len(parts)):
                gather(mask, b, part).wait_recv()
    for mask in range(1, n):
        share_power(mask).wait_send()
    for off in range(1, subs):
        share_sub(off).wait_send()


def regroup_plan(n, subs, mantissas, exponents, channel, inverses):
    _, blocks, vectors, ants = mantissas.shape
    users = channel.shape[4]
    width = 2 * users
    per = blocks // n
    parts = len(row_parts(vectors))
    flops = 2 * blocks * vectors * width * (ants + ITERS * width)
    dma = pltpu.SemaphoreType.DMA
    consensus, factor = pl.pallas_call(
        functools.partial(kernel, n, subs),
        out_shape=(
            jax.ShapeDtypeStruct((blocks, vectors, width), jnp.bfloat16),
            jax.ShapeDtypeStruct((1, width), jnp.float32),
        ),
        in_specs=[
            pl.BlockSpec(memory_space=pl.ANY),
            pl.BlockSpec(memory_space=pltpu.VMEM),
            pl.BlockSpec(memory_space=pl.ANY),
            pl.BlockSpec(memory_space=pl.ANY),
        ],
        out_specs=(
            pl.BlockSpec(memory_space=pltpu.VMEM),
            pl.BlockSpec(memory_space=pltpu.VMEM),
        ),
        scratch_shapes=[
            pltpu.VMEM((blocks, vectors, ants), jnp.int32),
            pltpu.VMEM((blocks, vectors, ants), jnp.bfloat16),
            pltpu.VMEM((n, per, vectors, ants), jnp.bfloat16),
            pltpu.VMEM((n, per) + channel.shape[2:], jnp.bfloat16),
            pltpu.VMEM((n, per) + inverses.shape[2:], jnp.bfloat16),
            pltpu.VMEM((n, ants, width), jnp.bfloat16),
            pltpu.VMEM((n, width, width), jnp.bfloat16),
            pltpu.VMEM((n, vectors, width), jnp.float32),
            pltpu.VMEM((n, vectors, width), jnp.float32),
            pltpu.VMEM((vectors, width), jnp.float32),
            pltpu.VMEM((1, users), jnp.float32),
            pltpu.VMEM((n, 1, users), jnp.float32),
            pltpu.VMEM((subs, 1, users), jnp.float32),
            dma,
            dma((2, per)),
            dma((2 + parts, n, per)),
            dma((2 + parts, n, per)),
            dma((parts, n, per)),
            dma((parts, n, per)),
            dma((n,)),
            dma((n,)),
            dma((subs,)),
            dma((subs,)),
        ],
        compiler_params=pltpu.CompilerParams(
            collective_id=0, has_side_effects=True, vmem_limit_bytes=60 * 1024 * 1024
        ),
        cost_estimate=pl.CostEstimate(flops=flops, bytes_accessed=8 * blocks * vectors * width, transcendentals=0),
    )(mantissas, exponents, channel, inverses)
    return (consensus.astype(jnp.float32) * factor[None]).astype(jnp.bfloat16)


def solution(mesh):
    n, subs = mesh.shape["cluster"], mesh.shape["sub"]

    def per_device(mantissas, exponents, channel, inverses):
        blocks = mantissas.shape[1]
        if n > 1 and n & (n - 1) == 0 and blocks % n == 0:
            return regroup_plan(n, subs, mantissas, exponents, channel, inverses)
        return reduce_plan(mantissas, exponents, channel, inverses)

    placed = (
        P("cluster", "sub", None, None),
        P("cluster", "sub", None),
        P("cluster", "sub", None, None, None),
        P("cluster", "sub", None, None, None),
    )
    return jax.shard_map(
        per_device, mesh=mesh, in_specs=placed, out_specs=P("sub", None, None), check_vma=False
    )
```

time: 91.3 us -> 83.3 us (0.912)
  Pallas kernels: 85.3 us -> 79 us
  local copies, waits for them, and re-layouts: 4.37 us -> 1.37 us
  other arithmetic: 1.4 us -> 2.69 us
    pallas_call x1, Pallas kernels: 85.3 us -> 79 us  [regroup_plan(): pl.pallas_call(functools.partial(kernel, n, subs), out_shape=(jax.ShapeDt...]
    unnamed x7 -> x1, local copies, waits for them, and re-layouts: 4.37 us -> 1.37 us
    convert_element_type x1, other arithmetic: 1.4 us -> 2.69 us  [regroup_plan(): return (consensus.astype(jnp.float32) * factor[None]).astype(jnp.bfloat16)]
where the time goes in v2:
time: 83.3 us; the launch traced here: 83.1 us
  Pallas kernels  79 us (95%)
  other arithmetic  2.69 us (3%)
  local copies, waits for them, and re-layouts  1.37 us (2%)
    pallas_call x1, Pallas kernels, regroup_plan(): pl.pallas_call(functools.partial(kernel, n, subs), out_shape=(jax.ShapeDt...  79 us
    convert_element_type x1, other arithmetic, regroup_plan(): return (consensus.astype(jnp.float32) * factor[None]).astype(jnp.bfloat16)  2.69 us

profile of v2, /device:TPU:0, one launch (start us, length us, event | category | flops | bytes accessed | tf_op | source)
XLA Modules:
  0.0 83.1 jit_solution(11921926640533015965)
XLA Ops:
  0.0 1.4 %copy.5.expo_ref = s32[1,16,14]{2,1,0:T(8,128)} copy(s32[1,16,14]{1,0,2:T(1,128)} %param.5) | data formatting | bytes 1792 | tf_op args[1]
  1.4 79.0 %shard_map.46 = (bf16[16,168,256]{2,1,0:T(8,128)(2,1)}, f32[1,256]{1,0:T(1,128)}) custom-call(s32[1,16,168,128]{3,2,1,0:T(8,128)} %mant_hbm.1, s32[1,16,14]{2,1,0:T(8,128)} %copy.5.expo_ref, bf16[1,16,2,64,128]{4,3,2,1,0:T(8,128)(2,1)} %chan_hbm.1, bf16[1,16,2,128,128]{4,3,2,1,0:T(8,128)(2,1)} %inv_hbm.1), custom_call_target="tpu_custom_call" | custom-call | flops 1233125376 | bytes 5505024 | tf_op jit(solution)/shard_map/pallas_call | solution.py:290
  80.4 2.7 %multiply_convert_fusion = bf16[16,168,256]{2,1,0:T(8,128)(2,1)} fusion(bf16[16,168,256]{2,1,0:T(8,128)(2,1)} %get-tuple-element.7, f32[256]{0:T(256)} %bitcast.1), kind=kLoop, calls=%fused_computation | loop fusion | flops 2064384 | bytes 2753536 | tf_op jit(solution)/shard_map/convert_element_type | solution.py:336

commit v3 on v2

--- a/solution.py
+++ b/solution.py
@@ -181,6 +181,15 @@
         return lax.dot_general(
             rhs.astype(jnp.bfloat16), solve_v[c], (((1,), (1,)), ((), ())), preferred_element_type=jnp.float32
         )
+
+    def relay(masks, b, part):
+        if part > 0:
+            pass_on(masks, b, part - 1)
+        else:
+
+            @pl.when(b > 0)
+            def _():
+                pass_on(masks, b - 1, len(parts) - 1)
 
     def one_slot(b, carry):
         for part, (at, count) in enumerate(parts):
@@ -215,11 +224,9 @@
                 term_v[c, rows] = term
                 total = term if total is None else total + term
 
-            @pl.when(b > 0)
-            def _():
-                pass_on(early, b - 1, part)
-
             for step in range(1, ITERS):
+                if step == ITERS - 1:
+                    relay(early, b, part)
                 cons_v[rows] = (total / n).astype(jnp.bfloat16).astype(jnp.float32)
                 total = None
                 for c in range(n):
@@ -231,33 +238,33 @@
                     total = term if total is None else total + term
             done = (total / n).astype(jnp.bfloat16)
             out_ref[me * per + b, rows] = done
-            for bit in reversed(range(bits)):
-                gather(2**bit, b, part).start()
             done = done.astype(jnp.float32)
             columns = jnp.sum(done * done, axis=0, keepdims=True)
             power_v[...] += columns[:, :users] + columns[:, users:]
-
-            @pl.when(b > 0)
-            def _():
-                pass_on(late, b - 1, part)
+            if part == len(parts) - 1:
+
+                @pl.when(b == per - 1)
+                def _():
+                    r_pow[me] = power_v[...]
+                    for mask in order:
+                        share_power(mask).start()
+
+            for bit in reversed(range(bits)):
+                gather(2**bit, b, part).start()
+            relay(late, b, part)
 
         return carry
 
     lax.fori_loop(0, per, one_slot, 0)
 
-    r_pow[me] = power_v[...]
-    for mask in range(1, n):
-        share_power(mask).start()
     last = per - 1
-    for part in range(len(parts)):
-        pass_on(early, last, part)
+    pass_on(early, last, len(parts) - 1)
     for mask in range(1, n):
         share_power(mask).wait_recv()
     r_sub[my_sub] = jnp.sum(r_pow[...], axis=0)
     for off in range(1, subs):
         share_sub(off).start()
-    for part in range(len(parts)):
-        pass_on(late, last, part)
+    pass_on(late, last, len(parts) - 1)
     for off in range(1, subs):
         share_sub(off).wait_recv()
     power = jnp.sum(r_sub[...], axis=0) / (blocks * subs * vectors)
@@ -294,10 +301,10 @@
             jax.ShapeDtypeStruct((1, width), jnp.float32),
         ),
         in_specs=[
-            pl.BlockSpec(memory_space=pl.ANY),
+            pl.BlockSpec(memory_space=pltpu.HBM),
             pl.BlockSpec(memory_space=pltpu.VMEM),
-            pl.BlockSpec(memory_space=pl.ANY),
-            pl.BlockSpec(memory_space=pl.ANY),
+            pl.BlockSpec(memory_space=pltpu.HBM),
+            pl.BlockSpec(memory_space=pltpu.HBM),
         ],
         out_specs=(
             pl.BlockSpec(memory_space=pltpu.VMEM),

time: 83.3 us -> 87.9 us (1.055)
  Pallas kernels: 79 us -> 83.6 us
    pallas_call x1, Pallas kernels: 79 us -> 83.6 us  [regroup_plan(): pl.pallas_call(functools.partial(kernel, n, subs), out_shape=(jax.ShapeDt...]
where the time goes in v3:
time: 87.9 us; the launch traced here: 87.7 us
  Pallas kernels  83.6 us (95%)
  other arithmetic  2.69 us (3%)
  local copies, waits for them, and re-layouts  1.37 us (2%)
    pallas_call x1, Pallas kernels, regroup_plan(): pl.pallas_call(functools.partial(kernel, n, subs), out_shape=(jax.ShapeDt...  83.6 us
    convert_element_type x1, other arithmetic, regroup_plan(): return (consensus.astype(jnp.float32) * factor[None]).astype(jnp.bfloat16)  2.69 us

profile of v3, /device:TPU:0, one launch (start us, length us, event | category | flops | bytes accessed | tf_op | source)
XLA Modules:
  0.0 87.7 jit_solution(6252147310216690382)
XLA Ops:
  0.0 1.4 %copy.5.expo_ref = s32[1,16,14]{2,1,0:T(8,128)} copy(s32[1,16,14]{1,0,2:T(1,128)} %param.5) | data formatting | bytes 1792 | tf_op args[1]
  1.4 83.6 %shard_map.46 = (bf16[16,168,256]{2,1,0:T(8,128)(2,1)}, f32[1,256]{1,0:T(1,128)}) custom-call(s32[1,16,168,128]{3,2,1,0:T(8,128)} %mant_hbm.1, s32[1,16,14]{2,1,0:T(8,128)} %copy.5.expo_ref, bf16[1,16,2,64,128]{4,3,2,1,0:T(8,128)(2,1)} %chan_hbm.1, bf16[1,16,2,128,128]{4,3,2,1,0:T(8,128)(2,1)} %inv_hbm.1), custom_call_target="tpu_custom_call" | custom-call | flops 1233125376 | bytes 5505024 | tf_op jit(solution)/shard_map/pallas_call | solution.py:297
  85.0 2.7 %multiply_convert_fusion = bf16[16,168,256]{2,1,0:T(8,128)(2,1)} fusion(bf16[16,168,256]{2,1,0:T(8,128)(2,1)} %get-tuple-element.7, f32[256]{0:T(256)} %bitcast.1), kind=kLoop, calls=%fused_computation | loop fusion | flops 2064384 | bytes 2753536 | tf_op jit(solution)/shard_map/convert_element_type | solution.py:343
